TPU v7x, 32 devices: a whole 2x2x4 slice. The times are simulated.
32 devices in a mesh: section: 2 (over x), dp: 16 (over z, y, core).
Axes of the slice: x: 2, y: 2, z: 4, core: 2. Of those that a mesh axis runs over, the one named last changes fastest.
Arguments:
- grads: bfloat16 [32, 524288], P(('section', 'dp')), parts along dimension 0, may hold values from -6 to 6
- master: float32 [32, 32768], P(('section', 'dp')), parts along dimension 0, may hold values from -30 to 30
- first_moment: float32 [32, 32768], P(('section', 'dp')), parts along dimension 0, may hold values from -0.6 to 0.6
- second_moment: float32 [32, 32768], P(('section', 'dp')), parts along dimension 0, may hold values from 0.005 to 0.05
- perm: int32 [32], P('section'), parts along dimension 0, may hold values from 0 to 15, each once
- bounds: int32 [34], P('section'), parts along dimension 0, may hold values from 0 to 524288, as said below
Outputs:
- new_weights: bfloat16 [1048576], P('section'), parts along dimension 0
- new_master: float32 [32, 32768], P(('section', 'dp')), parts along dimension 0
- new_first: float32 [32, 32768], P(('section', 'dp')), parts along dimension 0
- new_second: float32 [32, 32768], P(('section', 'dp')), parts along dimension 0
- step_taken: float32 [32, 32768], P(('section', 'dp')), parts along dimension 0
There are 2 independent parts, one for each index of `section`. A program takes and returns all parts, laid end to end along the dimension named above; each array names one. Nothing has to cross between parts.
Inputs may be any that keep to these rules, and one draw needn't show every extreme that they name: `perm`: each device index appears exactly once. `bounds`: strictly increasing multiples of 128, the first 0 and the last 524288.
All inputs are finite; a program needn't handle non-finite values.
Results may differ from a plain program's by a relative error of at most 0.0004.
Values may be sent and summed in bfloat16 or wider, within the bound.
No kernel may reach another device: no remote copies, remote signals or barrier semaphores. Data moves between devices by JAX's collectives and lax.ppermute only.
A program may use at most 128 MiB of HBM per device.

v0:
```python
import jax
import jax.numpy as jnp
from jax import lax
from jax.sharding import PartitionSpec as P

beta_first = 0.9
beta_second = 0.999
first_fix = 1.0 - 0.9**10
second_fix = 1.0 - 0.999**10
adam_eps = 1e-06
norm_eps = 1e-06
decay_rate = 0.01
learn_rate = 0.01


def per_device(grads, master, first_moment, second_moment, perm, bounds):
    replica_count = lax.axis_size("dp")
    shard_len = master.shape[1]
    own_block = perm[lax.axis_index("dp")]
    positions = own_block * shard_len + jnp.arange(shard_len, dtype=jnp.int32)
    member = (positions[None, :] >= bounds[:-1, None]) & (positions[None, :] < bounds[1:, None])
    onehot = member.astype(jnp.float32)
    weight_part = jnp.dot(onehot, master[0] * master[0], precision=lax.Precision.HIGHEST)
    summed = lax.psum(grads[0].astype(jnp.float32), "dp")
    own_grad = (
        lax.dynamic_slice_in_dim(summed, own_block * shard_len, shard_len)[None, :] / replica_count
    )
    new_first = beta_first * first_moment + (1.0 - beta_first) * own_grad
    new_second = beta_second * second_moment + (1.0 - beta_second) * own_grad * own_grad
    direction = (
        new_first / first_fix / (jnp.sqrt(new_second / second_fix) + adam_eps) + decay_rate * master
    )
    update_part = jnp.dot(onehot, direction[0] * direction[0], precision=lax.Precision.HIGHEST)
    weight_sq, update_sq = lax.psum((weight_part, update_part), "dp")
    trust_ratio = jnp.sqrt(weight_sq) / (jnp.sqrt(update_sq) + norm_eps)
    entry_ratio = jnp.dot(trust_ratio, onehot, precision=lax.Precision.HIGHEST)
    step_taken = entry_ratio[None, :] * direction
    new_master = master - learn_rate * step_taken
    gathered = lax.all_gather(new_master.astype(jnp.bfloat16), "dp", axis=0, tiled=True)
    inverse = jnp.argsort(perm)
    new_weights = jnp.take(gathered, inverse, axis=0).reshape(-1)
    return (new_weights, new_master, new_first, new_second, step_taken)


def solution(mesh):
    return jax.shard_map(
        per_device,
        mesh=mesh,
        in_specs=(
            P(("section", "dp"), None),
            P(("section", "dp"), None),
            P(("section", "dp"), None),
            P(("section", "dp"), None),
            P("section"),
            P("section"),
        ),
        out_specs=(
            P("section"),
            P(("section", "dp"), None),
            P(("section", "dp"), None),
            P(("section", "dp"), None),
            P(("section", "dp"), None),
        ),
        check_vma=False,
    )
```

profile of v0, /device:TPU:0, one launch (start us, length us, event | category | flops | bytes accessed | tf_op | source)
XLA Modules:
  0.0 200.4 jit_solution(13734129077697938728)
XLA Ops:
  7.2 0.0 all-reduce.3.cloned.1.call-start
  7.2 4.8 %convert_element_type.13 = f32[1,524288]{1,0:T(1,128)} convert(bf16[1,524288]{1,0:T(2,128)(2,1)} %param.6) | non-fusion elementwise | flops 524288 | bytes 3145728 | tf_op jit(solution)/shard_map/convert_element_type | solution.py:24
  12.0 0.0 copy-start.3
  12.0 0.0 all-reduce.3.cloned.1.call-update
  12.0 0.0 all-gather.3.cloned.1.call-start
  12.1 0.6 copy-done.5
  12.7 0.6 dynamic_slice.6
  13.9 0.1 fusion.17
  14.0 1.6 fusion.2
  15.6 97.5 %all-reduce.3.cloned.1.call-done = f32[524288]{0:T(1024)} async-done(((f32[524288]{0:T(1024)}), f32[524288]{0:T(1024)}) %all-reduce.3.cloned.1.call-update) | async-done | bytes 2097168 | tf_op jit(solution)/shard_map/psum | solution.py:24
  113.1 0.9 multiply_multiply_fusion
  114.0 1.4 multiply_add_fusion
  115.4 1.6 fusion.3
  117.1 30.4 %all-reduce = (f32[16]{0:T(128)S(1)}, f32[16]{0:T(128)S(1)}) all-reduce(f32[16]{0:T(128)S(1)} %fusion.3, f32[16]{0:T(128)S(1)} %fusion.2), channel_id=1, replica_groups=mesh['section'=2,'dp'=16] {'dp'}, use_global_device_ids=true, to_apply=%region_3.0 | all-reduce | flops 32 | bytes 256 | tf_op jit(solution)/shard_map/psum | solution.py:34
  147.5 0.9 convolution_multiply_fusion
  148.4 0.0 copy-start.1
  148.4 0.9 convert_bitcast_fusion
  149.4 0.0 all-gather.3.cloned.1.call-update
  149.4 1.3 sort.17
  150.7 37.5 %all-gather.3.cloned.1.call-done = bf16[16,1,32768]{2,1,0:T(2,128)(2,1)} async-done(((bf16[1,1,32768]{2,1,0:T(2,128)(2,1)}), bf16[16,1,32768]{2,1,0:T(2,128)(2,1)}) %all-gather.3.cloned.1.call-update) | async-done | bytes 1048592 | tf_op jit(solution)/shard_map/all_gather | solution.py:39
  188.2 2.7 %copy.14 = bf16[16,1,32768]{2,0,1:T(8,128)(2,1)S(1)} copy(bf16[16,1,32768]{2,1,0:T(2,128)(2,1)} %all-gather.3.cloned.1.call-done) | data formatting | bytes 2097152
  191.0 1.2 gather_fusion
  192.2 0.2 select_bitcast_fusion
  192.4 1.2 copy.12
  (14 shorter events, 0.1 us)
Async XLA Ops:
  7.2 105.9 %all-reduce.3.cloned.1.call-start = ((), (), s32[]{:S(2)}) async-start(), calls=%async_computation | async-start | bytes 4194304 | tf_op jit(solution)/shard_map/psum | solution.py:24
  12.0 0.7 copy-start.5
  12.0 1.9 copy-start.4
  12.0 2.0 copy-start
  12.0 102.0 %copy-start.2 = (f32[1,32768]{1,0:T(1,128)S(1)}, f32[1,32768]{1,0:T(1,128)}, u32[]{:S(2)}) copy-start(f32[1,32768]{1,0:T(1,128)} %param.8) | copy-start | bytes 393220
  12.0 102.0 %copy-start.3 = (f32[1,32768]{1,0:T(1,128)S(1)}, f32[1,32768]{1,0:T(1,128)}, u32[]{:S(2)}) copy-start(f32[1,32768]{1,0:T(1,128)} %param.9) | copy-start | bytes 393220
  12.0 176.2 %all-gather.3.cloned.1.call-start = ((), (), s32[]{:S(2)}) async-start(), calls=%async_computation.1 | async-start | bytes 2228224 | tf_op jit(solution)/shard_map/all_gather | solution.py:39
  148.4 43.8 %copy-start.1 = (f32[1,32768]{1,0:T(1,128)}, f32[1,32768]{1,0:T(1,128)S(1)}, u32[]{:S(2)}) copy-start(f32[1,32768]{1,0:T(1,128)S(1)} %convolution_multiply_fusion) | copy-start | bytes 393220
Sparse Core Ops, SparseCore 0:
  12.2 100.8 all-reduce.2
  149.5 38.6 all-gather.2
where the time goes:
time: 201 us; the launch traced here: 200 us
  waiting for transfers between devices  135 us (67%)
  blocking collectives  30.4 us (15%)
  between operations  14.8 us (7%)
  other arithmetic  9.55 us (5%)
  local copies, waits for them, and re-layouts  6.37 us (3%)
  matrix products  4.16 us (2%)
    psum x1, waiting for transfers between devices, per_device(): summed = lax.psum(grads[0].astype(jnp.float32), 'dp')  97.5 us
    all_gather x1, waiting for transfers between devices, per_device(): lax.all_gather(new_master.astype(jnp.bfloat16), 'dp', axis=0, tiled=True)  37.5 us
    psum x1, blocking collectives, per_device(): weight_sq, update_sq = lax.psum((weight_part, update_part), 'dp')  30.4 us
    convert_element_type x1, other arithmetic, per_device(): summed = lax.psum(grads[0].astype(jnp.float32), 'dp')  4.79 us
    unnamed x14, local copies, waits for them, and re-layouts  4.48 us
  transfers between devices with their start and end apart: 2, of which 2 were waited for; matrix products, arithmetic and copies ran while one was open for 2% of the time, Pallas kernels for 0%

commit v1 on v0

--- a/solution.py
+++ b/solution.py
@@ -21,7 +21,7 @@
     member = (positions[None, :] >= bounds[:-1, None]) & (positions[None, :] < bounds[1:, None])
     onehot = member.astype(jnp.float32)
     weight_part = jnp.dot(onehot, master[0] * master[0], precision=lax.Precision.HIGHEST)
-    summed = lax.psum(grads[0].astype(jnp.float32), "dp")
+    summed = jnp.sum(lax.all_gather(grads[0].astype(jnp.float32), "dp"), axis=0)
     own_grad = (
         lax.dynamic_slice_in_dim(summed, own_block * shard_len, shard_len)[None, :] / replica_count
     )

time: 201 us -> 296 us (1.47)
  waiting for transfers between devices: 135 us -> 205 us
  other arithmetic: 9.55 us -> 33.2 us
    all_gather x0 -> x1, waiting for transfers between devices: none -> 167 us  [per_device(): summed = jnp.sum(lax.all_gather(grads[0].astype(jnp.float32), 'dp'), axis=0)]
    psum x1 -> x0, waiting for transfers between devices: 97.5 us -> none  [per_device(): summed = lax.psum(grads[0].astype(jnp.float32), 'dp')]
    reduce_sum x0 -> x1, other arithmetic: none -> 24.5 us  [per_device(): summed = jnp.sum(lax.all_gather(grads[0].astype(jnp.float32), 'dp'), axis=0)]
    unnamed x2 -> x3, other arithmetic: 1.1 us -> 5.92 us
    convert_element_type x1 -> x0, other arithmetic: 4.79 us -> none  [per_device(): summed = lax.psum(grads[0].astype(jnp.float32), 'dp')]
  transfers between devices with their start and end apart: 2 -> 2, of which waited for: 2 -> 2; matrix products, arithmetic and copies ran while one was open for 2% -> 1% of each run, Pallas kernels for 0% -> 0%
where the time goes in v1:
time: 296 us
  waiting for transfers between devices  205 us (69%)
  other arithmetic  33.2 us (11%)
  blocking collectives  32.6 us (11%)
  between operations  14.8 us (5%)
  local copies, waits for them, and re-layouts  6.41 us (2%)
  matrix products  4.16 us (1%)
    all_gather x1, waiting for transfers between devices, per_device(): summed = jnp.sum(lax.all_gather(grads[0].astype(jnp.float32), 'dp'), axis=0)  167 us
    all_gather x1, waiting for transfers between devices, per_device(): lax.all_gather(new_master.astype(jnp.bfloat16), 'dp', axis=0, tiled=True)  37.5 us
    psum x1, blocking collectives, per_device(): weight_sq, update_sq = lax.psum((weight_part, update_part), 'dp')  32.6 us
    reduce_sum x1, other arithmetic, per_device(): summed = jnp.sum(lax.all_gather(grads[0].astype(jnp.float32), 'dp'), axis=0)  24.5 us
    unnamed x3, other arithmetic  5.92 us
  transfers between devices with their start and end apart: 2, of which 2 were waited for; matrix products, arithmetic and copies ran while one was open for 1% of the time, Pallas kernels for 0%

profile of v1, /device:TPU:0, one launch (start us, length us, event | category | flops | bytes accessed | tf_op | source)
XLA Modules:
  0.0 296.2 jit_solution(17132078166889588620)
XLA Ops:
  7.2 0.0 all-gather.5.cloned.1.call-start
  7.2 4.8 %bitcast_convert_fusion = f32[1,1,524288]{2,1,0:T(1,128)} fusion(bf16[1,524288]{1,0:T(2,128)(2,1)} %param.6), kind=kLoop, calls=%fused_computation.2 | loop fusion | flops 524288 | bytes 3145728
  12.0 0.0 all-gather.5.cloned.1.call-update
  12.0 0.0 all-gather.7.cloned.1.call-start
  12.1 0.6 copy-done.5
  12.7 0.6 dynamic_slice.6
  13.9 0.1 fusion.17
  14.0 1.6 fusion.2
  15.6 0.0 copy-start.2
  15.7 167.3 %all-gather.5.cloned.1.call-done = f32[16,1,524288]{2,1,0:T(1,128)} async-done(((f32[1,1,524288]{2,1,0:T(1,128)}), f32[16,1,524288]{2,1,0:T(1,128)}) %all-gather.5.cloned.1.call-update) | async-done | bytes 33554448 | tf_op jit(solution)/shard_map/all_gather | solution.py:24
  183.0 24.5 %reduce_sum.9 = f32[524288]{0:T(1024)S(1)} reduce(f32[16,1,524288]{2,1,0:T(1,128)} %all-gather.5.cloned.1.call-done, f32[]{:T(128)} %constant.13.clone.1), dimensions={0,1}, to_apply=%region_2.0 | reduce | flops 7864320 | bytes 35651588 | tf_op jit(solution)/shard_map/reduce_sum | solution.py:24
  207.6 1.4 multiply_add_fusion
  209.0 1.6 fusion.3
  210.6 32.6 %all-reduce = (f32[16]{0:T(128)S(1)}, f32[16]{0:T(128)S(1)}) all-reduce(f32[16]{0:T(128)S(1)} %fusion.3, f32[16]{0:T(128)S(1)} %fusion.2), channel_id=1, replica_groups=mesh['section'=2,'dp'=16] {'dp'}, use_global_device_ids=true, to_apply=%region_3.0 | all-reduce | flops 32 | bytes 256 | tf_op jit(solution)/shard_map/psum | solution.py:34
  243.2 0.9 convolution_multiply_fusion
  244.2 0.0 copy-start.1
  244.2 1.0 convert_bitcast_fusion
  245.1 0.0 all-gather.7.cloned.1.call-update
  245.2 1.3 sort.17
  246.5 37.5 %all-gather.7.cloned.1.call-done = bf16[16,1,32768]{2,1,0:T(2,128)(2,1)} async-done(((bf16[1,1,32768]{2,1,0:T(2,128)(2,1)}), bf16[16,1,32768]{2,1,0:T(2,128)(2,1)}) %all-gather.7.cloned.1.call-update) | async-done | bytes 1048592 | tf_op jit(solution)/shard_map/all_gather | solution.py:39
  284.0 2.7 copy.14
  286.7 1.2 gather_fusion
  288.0 0.2 select_bitcast_fusion
  288.2 1.2 copy.12
  (15 shorter events, 0.1 us)
Async XLA Ops:
  7.2 175.8 %all-gather.5.cloned.1.call-start = ((), (), s32[]{:S(2)}) async-start(), calls=%async_computation | async-start | bytes 35651584 | tf_op jit(solution)/shard_map/all_gather | solution.py:24
  12.0 0.7 copy-start.5
  12.0 1.9 copy-start.4
  12.0 2.0 copy-start
  12.0 271.9 %all-gather.7.cloned.1.call-start = ((), (), s32[]{:S(2)}) async-start(), calls=%async_computation.1 | async-start | bytes 2228224 | tf_op jit(solution)/shard_map/all_gather | solution.py:39
  15.6 191.9 %copy-start.2 = (f32[1,32768]{1,0:T(1,128)S(1)}, f32[1,32768]{1,0:T(1,128)}, u32[]{:S(2)}) copy-start(f32[1,32768]{1,0:T(1,128)} %param.8) | copy-start | bytes 393220
  15.7 191.9 %copy-start.3 = (f32[1,32768]{1,0:T(1,128)S(1)}, f32[1,32768]{1,0:T(1,128)}, u32[]{:S(2)}) copy-start(f32[1,32768]{1,0:T(1,128)} %param.9) | copy-start | bytes 393220
  244.2 43.8 %copy-start.1 = (f32[1,32768]{1,0:T(1,128)}, f32[1,32768]{1,0:T(1,128)S(1)}, u32[]{:S(2)}) copy-start(f32[1,32768]{1,0:T(1,128)S(1)} %convolution_multiply_fusion) | copy-start | bytes 393220
Sparse Core Ops, SparseCore 0:
  12.2 170.7 all-gather.4
  245.3 38.6 all-gather.6
